TPU v7x, 256 devices: a whole 4x4x8 slice. The times are simulated.
256 devices in a mesh: dp: 32 (over z, y), tensor: 8 (over x, core).
Axes of the slice: x: 4, y: 4, z: 8, core: 2. Of those that a mesh axis runs over, the one named last changes fastest.
Arguments:
- layer_outs: bfloat16 [5, 32768, 4096], P(None, 'dp', 'tensor'), may hold values from -6 to 6
- avg_grads: bfloat16 [4, 32768, 4096], P(None, 'dp', 'tensor'), may hold values from -0.00051498413 to 0.00051498413
- attn_mixed: bfloat16 [32768, 4096], P('dp', 'tensor'), may hold values from -96 to 96
- dwa_coefs: float32 [4, 5], replicated, may hold values from -1.5 to 1.5
Outputs:
- coef_grad: float32 [4, 5], replicated
- proj_grad: float32 [4096, 4096], P('dp', 'tensor')
All inputs are finite; a program needn't handle non-finite values.
Results may differ from a plain program's by a relative error of at most 0.0042.
Values may be sent and summed in bfloat16 or wider, within the bound.
A program may use at most 64 MiB of HBM per device.

v0:
```python
import jax
import jax.numpy as jnp
from jax import lax
from jax.sharding import PartitionSpec as P


def copy_for_each(value, axis):
    length = lax.axis_size(axis)
    return lax.all_to_all(
        jnp.broadcast_to(value[None], (length, *value.shape)), axis, 0, 0, tiled=True
    )


def over_copies(value, axis):
    everything = copy_for_each(value, axis)
    return jnp.sum(everything, axis=0)


def split_up(value, dim, length):
    before, after = (value.shape[:dim], value.shape[dim + 1 :])
    return jnp.moveaxis(value.reshape(*before, length, -1, *after), dim, 0)


def sum_at_owner(value, axis, dim):
    length = lax.axis_size(axis)
    parts = lax.all_to_all(split_up(value, dim, length), axis, 0, 0, tiled=True)
    return jnp.sum(parts.astype(jnp.float32), axis=0)


def coef_partial(layer_outs, avg_grads):
    depth = avg_grads.shape[0]
    grads_flat = avg_grads.reshape(depth, -1)
    outs_flat = layer_outs.reshape(depth + 1, -1)
    return lax.dot_general(
        grads_flat, outs_flat, (((1,), (1,)), ((), ())), preferred_element_type=jnp.float32
    )


def coef_total(partial_sum):
    across = over_copies(partial_sum, "tensor")
    return over_copies(across, "dp")


def coef_masked(raw):
    depth = raw.shape[0]
    rows = jnp.arange(depth, dtype=jnp.int32)[:, None]
    cols = jnp.arange(depth + 1, dtype=jnp.int32)[None, :]
    return jnp.where(cols <= rows + 1, raw, jnp.float32(0.0))


def weight_grad(avg_grads, attn_mixed, dwa_coefs):
    depth = avg_grads.shape[0]
    first = dwa_coefs[depth - 2, depth - 1] * avg_grads[depth - 2].astype(jnp.float32)
    second = dwa_coefs[depth - 1, depth - 1] * avg_grads[depth - 1].astype(jnp.float32)
    out_grad = (first + second).astype(jnp.bfloat16)
    term = lax.dot_general(
        lax.all_gather(out_grad, "tensor", axis=1, tiled=True),
        attn_mixed,
        (((0,), (0,)), ((), ())),
        preferred_element_type=jnp.float32,
    )
    return sum_at_owner(term.astype(jnp.bfloat16), "dp", 0)


def local(layer_outs, avg_grads, attn_mixed, dwa_coefs):
    partial_sum = coef_partial(layer_outs, avg_grads)
    proj_grad = weight_grad(avg_grads, attn_mixed, dwa_coefs)
    raw = coef_total(partial_sum)
    return (coef_masked(raw), proj_grad)


def solution(mesh):
    in_specs = (P(None, "dp", "tensor"), P(None, "dp", "tensor"), P("dp", "tensor"), P())
    out_specs = (P(), P("dp", "tensor"))
    return jax.shard_map(local, mesh=mesh, in_specs=in_specs, out_specs=out_specs, check_vma=False)
```

profile of v0, /device:TPU:4, one launch (start us, length us, event | category | flops | bytes accessed | tf_op | source)
XLA Modules:
  0.0 193.6 jit_solution(11887079375010073203)
XLA Ops:
  7.2 0.0 copy-start
  7.2 0.0 all-gather.3.cloned.1.call-start
  7.2 1.4 fusion.14
  8.6 4.3 %add_convert_fusion = bf16[1,1024,512]{2,1,0:T(8,128)(2,1)} fusion(bf16[4,1024,512]{2,1,0:T(8,128)(2,1)} %param.5, f32[]{:T(128)} %bitcast.2, f32[]{:T(128)} %bitcast.1), kind=kLoop, calls=%fused_computation.7 | loop fusion | flops 3145728 | bytes 3145736 | tf_op jit(solution)/shard_map/convert_element_type | solution.py:55
  12.9 0.0 all-gather.3.cloned.1.call-update
  12.9 12.0 %fusion.8 = f32[4,5]{1,0:T(4,128)S(1)} fusion(bf16[5,1024,512]{2,1,0:T(8,128)(2,1)} %param.4, bf16[4,1024,512]{2,1,0:T(8,128)(2,1)} %param.5), kind=kOutput, calls=%fused_computation.8 | convolution fusion | flops 20971520 | bytes 9437264 | tf_op jit(solution)/shard_map/dot_general | solution.py:34
  24.9 7.6 %all_to_all.15 = f32[8,4,5]{2,1,0:T(4,128)S(1)} all-to-all(f32[8,4,5]{2,1,0:T(4,128)S(1)} %broadcast_in_dim.7), channel_id=1, replica_groups=mesh['dp'=32,'tensor'=8] {'tensor'}, dimensions={0} | all-to-all | bytes 1280 | tf_op jit(solution)/shard_map/all_to_all | solution.py:9
  32.4 0.6 broadcast_in_dim.8
  33.1 11.7 %all-to-all-start.1 = ((f32[32,4,5]{2,1,0:T(4,128)}), f32[32,4,5]{2,1,0:T(4,128)S(1)}, u32[]{:S(2)}, u32[]{:S(2)}) async-start(f32[32,4,5]{2,1,0:T(4,128)} %broadcast_in_dim.8), calls=%async_computation.1 | async-start | bytes 131072 | tf_op jit(solution)/shard_map/all_to_all | solution.py:9
  44.8 22.5 %all-gather.3.cloned.1.call-done = bf16[1,1024,4096]{2,1,0:T(8,128)(2,1)} async-done(((bf16[1,1024,512]{2,1,0:T(8,128)(2,1)}), bf16[1,1024,4096]{2,1,0:T(8,128)(2,1)}) %all-gather.3.cloned.1.call-update) | async-done | bytes 8388624 | tf_op jit(solution)/shard_map/all_gather | solution.py:57
  67.3 0.0 copy-done
  67.3 9.7 %fusion.4 = bf16[4096,512]{1,0:T(8,128)(2,1)} fusion(bf16[1024,512]{1,0:T(8,128)(2,1)S(1)} %copy-done, bf16[1,1024,4096]{2,1,0:T(8,128)(2,1)} %all-gather.3.cloned.1.call-done), kind=kOutput, calls=%fused_computation.5 | convolution fusion | flops 4297064448 | bytes 13631488 | tf_op jit(solution)/shard_map/dot_general | solution.py:56
  77.0 0.0 all-to-all-done.1
  77.0 10.0 %all-to-all-start.2 = ((bf16[32,128,512]{2,1,0:T(8,128)(2,1)}), bf16[32,128,512]{2,1,0:T(8,128)(2,1)}, u32[]{:S(2)}, u32[]{:S(2)}) async-start(bf16[32,128,512]{2,1,0:T(8,128)(2,1)} %bitcast.11), calls=%async_computation.2 | async-start | bytes 8388608 | tf_op jit(solution)/shard_map/all_to_all | solution.py:26
  87.0 0.1 copy.25
  87.1 0.7 copy.23
  87.8 95.4 %all-to-all-done.2 = bf16[32,128,512]{2,1,0:T(8,128)(2,1)} async-done(((bf16[32,128,512]{2,1,0:T(8,128)(2,1)}), bf16[32,128,512]{2,1,0:T(8,128)(2,1)}, u32[]{:S(2)}, u32[]{:S(2)}) %all-to-all-start.2) | async-done | bytes 4194336 | tf_op jit(solution)/shard_map/all_to_all | solution.py:26
  183.3 3.5 %convert_reduce_fusion = f32[128,512]{1,0:T(8,128)} fusion(bf16[32,128,512]{2,1,0:T(8,128)(2,1)} %all-to-all-done.2), kind=kLoop, calls=%fused_computation.4 | loop fusion | flops 4128768 | bytes 4456448 | tf_op jit(solution)/shard_map/reduce_sum | solution.py:27
  (5 shorter events, 0.1 us)
Async XLA Ops:
  7.2 60.1 %copy-start = (bf16[1024,512]{1,0:T(8,128)(2,1)S(1)}, bf16[1024,512]{1,0:T(8,128)(2,1)}, u32[]{:S(2)}) copy-start(bf16[1024,512]{1,0:T(8,128)(2,1)} %param.6) | copy-start | bytes 3145732
  7.2 60.1 %all-gather.3.cloned.1.call-start = ((), (), s32[]{:S(2)}) async-start(), calls=%async_computation.3 | async-start | bytes 9437184 | tf_op jit(solution)/shard_map/all_gather | solution.py:57
  33.1 43.9 %all-to-all-start.1 = ((f32[32,4,5]{2,1,0:T(4,128)}), f32[32,4,5]{2,1,0:T(4,128)S(1)}, u32[]{:S(2)}, u32[]{:S(2)}) async-start(f32[32,4,5]{2,1,0:T(4,128)} %broadcast_in_dim.8), calls=%async_computation.1 | async-start | bytes 131072 | tf_op jit(solution)/shard_map/all_to_all | solution.py:9
  77.0 106.3 %all-to-all-start.2 = ((bf16[32,128,512]{2,1,0:T(8,128)(2,1)}), bf16[32,128,512]{2,1,0:T(8,128)(2,1)}, u32[]{:S(2)}, u32[]{:S(2)}) async-start(bf16[32,128,512]{2,1,0:T(8,128)(2,1)} %bitcast.11), calls=%async_computation.2 | async-start | bytes 8388608 | tf_op jit(solution)/shard_map/all_to_all | solution.py:26
Sparse Core Ops, SparseCore 0:
  13.0 54.1 all-gather.2
where the time goes:
time: 197 us; the launch traced here: 194 us
  waiting for transfers between devices  118 us (60%)
  starting transfers between devices  21.7 us (11%)
  matrix products  21.7 us (11%)
  between operations  14.1 us (7%)
  other arithmetic  7.86 us (4%)
  blocking collectives  7.57 us (4%)
  local copies, waits for them, and re-layouts  2.78 us (1%)
    all_to_all x1, waiting for transfers between devices, sum_at_owner(): parts = lax.all_to_all(split_up(value, dim, length), axis, 0, 0, tiled=True)  95.4 us
    all_gather x1, waiting for transfers between devices, weight_grad(): lax.all_gather(out_grad, 'tensor', axis=1, tiled=True)  22.5 us
    dot_general x1, matrix products, coef_partial(): lax.dot_general(grads_flat, outs_flat, (((1,), (1,)), ((), ())), preferre...  12 us
    all_to_all x1, starting transfers between devices, copy_for_each(): lax.all_to_all(jnp.broadcast_to(value[None], (length, *value.shape)), axi...  11.7 us
    all_to_all x1, starting transfers between devices, sum_at_owner(): parts = lax.all_to_all(split_up(value, dim, length), axis, 0, 0, tiled=True)  9.99 us
    dot_general x1, matrix products, weight_grad(): lax.dot_general(lax.all_gather(out_grad, 'tensor', axis=1, tiled=True), a...  9.72 us
    all_to_all x1, blocking collectives, copy_for_each(): lax.all_to_all(jnp.broadcast_to(value[None], (length, *value.shape)), axi...  7.57 us
    convert_element_type x1, other arithmetic, weight_grad(): out_grad = (first + second).astype(jnp.bfloat16)  4.28 us
  transfers between devices with their start and end apart: 3, of which 2 were waited for; matrix products, arithmetic and copies ran while one was open for 12% of the time, Pallas kernels for 0%

commit v1 on v0

v1 whole, which is shorter than its diff:
```python
import jax
import jax.numpy as jnp
from jax import lax
from jax.experimental import pallas as pl
from jax.experimental.pallas import tpu as pltpu
from jax.sharding import PartitionSpec as P

MESH = pl.DeviceIdType.MESH
F32, BF16 = jnp.float32, jnp.bfloat16
NX, NY, NZ = 4, 4, 8
PAIRS = [(i, j) for i in range(4) for j in range(5) if j <= i + 1]


def kernel(
    co, lo_h, ag_h, at_h, coef_out, proj_out,
    lo, ag, ab, gt, pf, s1, r1, s2, r2, zs, zr, zsum, outb, cb_c, cb_x, cb_y, cb_z,
    in_sem, gd_s, gd_r, gx_s, gx_r, gf_s, gf_r, ax_s, ax_r,
    y1_s, y1_r, y2_s, y2_r, z_s, z_r, f_s, f_r, c_s, c_r,
):
    dp, tk = lax.axis_index("dp"), lax.axis_index("tensor")
    z, y = dp // NY, dp % NY
    x, c = tk // 2, tk % 2
    xg = x + 1 - 2 * (x % 2)
    xa = NX - 1 - x

    def dev(x_, y_, z_, c_):
        return (z_ * NY + y_, x_ * 2 + c_)

    def send(src, dst, send_sem, recv_sem, where):
        copy = pltpu.make_async_remote_copy(
            src_ref=src, dst_ref=dst, send_sem=send_sem, recv_sem=recv_sem,
            device_id=where, device_id_type=MESH,
        )
        copy.start()

    def arrived(ref, sem):
        pltpu.make_async_copy(ref, ref, sem).wait()

    others_x = [(x + k) % NX for k in range(1, NX)]
    others_y = [(y + k) % NY for k in range(1, NY)]
    others_z = [(z + k) % NZ for k in range(1, NZ)]

    loads = {}

    def load(name, src, dst, i):
        loads[name] = pltpu.make_async_copy(src, dst, in_sem.at[i])
        loads[name].start()

    load("ag2", ag_h.at[2], ag.at[2], 0)
    load("ag3", ag_h.at[3], ag.at[3], 1)
    load("ab0", at_h.at[:, pl.ds(0, 256)], ab.at[0], 2)
    load("ab1", at_h.at[:, pl.ds(256, 256)], ab.at[1], 3)
    load("ag0", ag_h.at[0], ag.at[0], 4)
    load("ag1", ag_h.at[1], ag.at[1], 5)
    for j in range(5):
        load(f"lo{j}", lo_h.at[j], lo.at[j], 6 + j)

    barrier = pltpu.get_barrier_semaphore()
    greeted = [dev(x, y, z, 1 - c)]
    greeted += [dev(x_, y, z, c) for x_ in others_x]
    greeted += [dev(x, y_, z, c) for y_ in others_y]
    greeted += [dev(x, y, z_, c) for z_ in others_z]
    greeted += [dev(xa, y, z_, c) for z_ in others_z]
    for where in greeted:
        pl.semaphore_signal(barrier, inc=1, device_id=where, device_id_type=MESH)

    loads["ag2"].wait()
    loads["ag3"].wait()
    c2, c3 = co[2, 3], co[3, 3]

    def out_grad(i, _):
        rows = pl.ds(pl.multiple_of(i * 256, 256), 256)
        for yy in range(NY):
            cols = pl.ds(yy * 128, 128)
            first = c2 * ag[2, rows, cols].astype(F32)
            second = c3 * ag[3, rows, cols].astype(F32)
            turned = (first + second).astype(BF16).T
            for hh in range(2):
                gt[hh, yy, c, :, rows] = turned[hh * 64 : hh * 64 + 64]
        return 0

    lax.fori_loop(0, 4, out_grad, 0)
    loads["ab0"].wait()
    loads["ab1"].wait()
    pl.semaphore_wait(barrier, len(greeted))

    for j in range(2):
        send(ab.at[j], ab.at[2 + j], ax_s.at[j], ax_r.at[j], dev(xa, y, z, c))
        send(gt.at[j, :, c], gt.at[2 + j, :, c], gx_s.at[j], gx_r.at[j], dev(xg, y, z, c))
        send(gt.at[j, :, c], gt.at[j, :, c], gd_s.at[j], gd_r.at[j], dev(x, y, z, 1 - c))

    up, down = dev(x, (y + 1) % NY, z, c), dev(x, (y + 3) % NY, z, c)

    def product(g, a):
        b = g * 4 + a

        def one(i, _):
            yc = (y + 2 + i) % NY
            term = jnp.dot(
                gt[g, yc].reshape(128, 1024), ab[a], preferred_element_type=F32
            )
            pf[b, yc] = term.reshape(8, 16, 256)
            return 0

        one(0, 0)
        far = pf[b, (y + 2) % NY].astype(BF16)
        s1[b, 0] = far[:, :, :128]
        s1[b, 1] = far[:, :, 128:]
        send(s1.at[b, 0], r1.at[b, 0], y1_s, y1_r.at[b, 0], up)
        send(s1.at[b, 1], r1.at[b, 1], y1_s, y1_r.at[b, 1], down)
        lax.fori_loop(1, NY, one, 0)

    def y_second(g, a):
        b = g * 4 + a
        arrived(r1.at[b, 0], y1_r.at[b, 0])
        yu = (y + 1) % NY
        s2[b, 0, :, :, :128] = (pf[b, yu, :, :, :128] + r1[b, 0].astype(F32)).astype(BF16)
        s2[b, 0, :, :, 128:] = pf[b, yu, :, :, 128:].astype(BF16)
        send(s2.at[b, 0], r2.at[b, 0], y2_s, y2_r.at[b, 0], up)
        arrived(r1.at[b, 1], y1_r.at[b, 1])
        yd = (y + 3) % NY
        s2[b, 1, :, :, :128] = pf[b, yd, :, :, :128].astype(BF16)
        s2[b, 1, :, :, 128:] = (pf[b, yd, :, :, 128:] + r1[b, 1].astype(F32)).astype(BF16)
        send(s2.at[b, 1], r2.at[b, 1], y2_s, y2_r.at[b, 1], down)

    def slot_of(z_, g):
        base = x + (xg - x) * (g // 2)
        return (z_ - 2 * base + 3 + NZ) % NZ, 2 * base

    def z_share(g, a):
        b = g * 4 + a
        arrived(r2.at[b, 0], y2_r.at[b, 0])
        arrived(r2.at[b, 1], y2_r.at[b, 1])
        total = pf[b, y] + r2[b, 0].astype(F32) + r2[b, 1].astype(F32)
        pf[b, y] = total
        zs[b] = total.astype(BF16)
        for k in range(1, NZ):
            there = (z + k) % NZ
            slot, _ = slot_of(there, g)
            send(zs.at[b, slot], zr.at[b, k - 1], z_s, z_r.at[b], dev(x, y, there, c))

    def to_home(g, a, own_plane):
        b = g * 4 + a
        arrived(zr.at[b], z_r.at[b])
        slot, home0 = slot_of(z, g)
        total = pf[b, y, slot]
        for k in range(NZ - 1):
            total = total + zr[b, k].astype(F32)
        zh = home0 + slot // 4
        block = (g % 2) * 4 + slot % 4
        if own_plane:

            @pl.when(zh == z)
            def _():
                outb[block, a % 2] = total

            @pl.when(zh != z)
            def _():
                zsum[b] = total
                send(zsum.at[b], outb.at[block, a % 2], f_s.at[b], f_r, dev(x, y, zh, c))

        else:
            zsum[b] = total
            send(zsum.at[b], outb.at[block, a % 2], f_s.at[b], f_r, dev(xa, y, zh, c))

    def run(fn, count, g_of, a_of, *more):
        def step(t, _):
            fn(g_of(t), a_of(t), *more)
            return 0

        lax.fori_loop(0, count, step, 0)

    first = (4, lambda t: t // 2, lambda t: t % 2)
    rows2, cols2 = (2, lambda t: 2, lambda t: t), (3, lambda t: t, lambda t: 2)
    rows3, cols3 = (3, lambda t: 3, lambda t: t), (4, lambda t: t, lambda t: 3)

    def all_to_home(shell, n):
        if shell == 0:
            run(to_home, 4, lambda t: t // 2, lambda t: t % 2, True)
        else:
            run(to_home, 2, lambda t: n, lambda t: t, True)
            run(to_home, n - 2, lambda t: n, lambda t: t + 2, False)
            run(to_home, n + 1, lambda t: t, lambda t: n, False)

    def features(j):
        arrived(gt.at[2 + j, :, c], gx_r.at[j])
        send(gt.at[2 + j, :, c], gt.at[2 + j, :, c], gf_s.at[j], gf_r.at[j], dev(x, y, z, 1 - c))
        arrived(gt.at[2 + j, :, 1 - c], gf_r.at[j])

    def coef_step(r, accs):
        rows = pl.ds(pl.multiple_of(r * 16, 16), 16)
        accs = list(accs)
        for q in range(4):
            cols = pl.ds(q * 128, 128)
            outs = [lo[j, rows, cols].astype(F32) for j in range(5)]
            grads = [ag[i, rows, cols].astype(F32) for i in range(4)]
            for n, (i, j) in enumerate(PAIRS):
                p = grads[i] * outs[j]
                accs[n] = accs[n] + (p[:8] + p[8:])
        return tuple(accs)

    def spread(buf, own, k0, targets, stage, size):
        for k, where in enumerate(targets):
            send(buf.at[own], buf.at[own], c_s.at[stage], c_r.at[stage], where)

    def settle(buf, own, stage, size):
        arrived(buf.at[pl.ds(0, size - 1)], c_r.at[stage])
        total = buf[0]
        for k in range(1, size):
            total = total + buf[k]
        return total

    def coef_local():
        for name in ["ag0", "ag1"] + [f"lo{j}" for j in range(5)]:
            loads[name].wait()
        zero = jnp.zeros((8, 128), F32)
        accs = lax.fori_loop(0, 64, coef_step, (zero,) * len(PAIRS))
        row = lax.broadcasted_iota(jnp.int32, (8, 128), 0)
        col = lax.broadcasted_iota(jnp.int32, (8, 128), 1)
        tile = zero
        for n, (i, j) in enumerate(PAIRS):
            total = jnp.sum(jnp.sum(accs[n], axis=0, keepdims=True), axis=1, keepdims=True)
            tile = jnp.where((row == i) & (col == j), jnp.broadcast_to(total, (8, 128)), tile)
        cb_c[c] = tile
        spread(cb_c, c, 0, [dev(x, y, z, 1 - c)], 0, 2)

    def coef_x():
        cb_x[x] = settle(cb_c, c, 0, 2)
        spread(cb_x, x, 0, [dev(x_, y, z, c) for x_ in others_x], 1, NX)

    def coef_y():
        cb_y[y] = settle(cb_x, x, 1, NX)
        spread(cb_y, y, 0, [dev(x, y_, z, c) for y_ in others_y], 2, NY)

    def coef_z():
        cb_z[z] = settle(cb_y, y, 2, NY)
        spread(cb_z, z, 0, [dev(x, y, z_, c) for z_ in others_z], 3, NZ)

    for j in range(2):
        arrived(gt.at[j, :, 1 - c], gd_r.at[j])
    run(product, *first)
    run(y_second, *first)
    coef_local()
    run(z_share, *first)
    coef_x()

    features(0)
    run(product, *rows2)
    arrived(ab.at[2], ax_r.at[0])
    run(product, *cols2)
    all_to_home(0, 0)
    coef_y()
    run(y_second, *rows2)
    run(y_second, *cols2)
    run(z_share, *rows2)
    run(z_share, *cols2)
    coef_z()

    features(1)
    run(product, *rows3)
    arrived(ab.at[3], ax_r.at[1])
    run(product, *cols3)
    all_to_home(1, 2)
    run(y_second, *rows3)
    run(y_second, *cols3)
    run(z_share, *rows3)
    run(z_share, *cols3)
    coef_out[...] = settle(cb_z, z, 3, NZ)[:4, :5]
    all_to_home(1, 3)

    at_home = z // 4 == x // 2

    @pl.when(at_home)
    def _():
        arrived(outb.at[pl.ds(0, 6)], f_r)

    @pl.when(jnp.logical_not(at_home))
    def _():
        arrived(outb, f_r)

    for block in range(8):
        for j in range(2):
            proj_out[pl.ds(block * 16, 16), pl.ds(j * 256, 256)] = outb[block, j]

    arrived(s1, y1_s)
    arrived(s2, y2_s)
    arrived(zr, z_s)
    for b in range(16):
        g, a = b // 4, b % 4
        if a < 2:
            slot, home0 = slot_of(z, g)

            @pl.when(home0 + slot // 4 != z)
            def _():
                arrived(zsum.at[b], f_s.at[b])

        else:
            arrived(zsum.at[b], f_s.at[b])
    arrived(cb_c.at[0], c_s.at[0])
    arrived(cb_x.at[pl.ds(0, NX - 1)], c_s.at[1])
    arrived(cb_y.at[pl.ds(0, NY - 1)], c_s.at[2])
    arrived(cb_z.at[pl.ds(0, NZ - 1)], c_s.at[3])
    for j in range(2):
        arrived(ab.at[j], ax_s.at[j])
        arrived(gt.at[j, :, c], gx_s.at[j])
        arrived(gt.at[j, :, c], gd_s.at[j])
        arrived(gt.at[2 + j, :, c], gf_s.at[j])


def local(layer_outs, avg_grads, attn_mixed, dwa_coefs):
    dma = pltpu.SemaphoreType.DMA
    anywhere = pl.BlockSpec(memory_space=pl.ANY)
    vmem = pl.BlockSpec(memory_space=pltpu.VMEM)
    return pl.pallas_call(
        kernel,
        out_shape=(
            jax.ShapeDtypeStruct((4, 5), F32),
            jax.ShapeDtypeStruct((128, 512), F32),
        ),
        in_specs=[pl.BlockSpec(memory_space=pltpu.SMEM), anywhere, anywhere, anywhere],
        out_specs=(vmem, vmem),
        scratch_shapes=[
            pltpu.VMEM((5, 1024, 512), BF16),
            pltpu.VMEM((4, 1024, 512), BF16),
            pltpu.VMEM((4, 1024, 256), BF16),
            pltpu.VMEM((4, NY, 2, 64, 1024), BF16),
            pltpu.VMEM((16, NY, 8, 16, 256), F32),
            pltpu.VMEM((16, 2, 8, 16, 128), BF16),
            pltpu.VMEM((16, 2, 8, 16, 128), BF16),
            pltpu.VMEM((16, 2, 8, 16, 256), BF16),
            pltpu.VMEM((16, 2, 8, 16, 256), BF16),
            pltpu.VMEM((16, 8, 16, 256), BF16),
            pltpu.VMEM((16, 7, 16, 256), BF16),
            pltpu.VMEM((16, 16, 256), F32),
            pltpu.VMEM((8, 2, 16, 256), F32),
            pltpu.VMEM((2, 8, 128), F32),
            pltpu.VMEM((NX, 8, 128), F32),
            pltpu.VMEM((NY, 8, 128), F32),
            pltpu.VMEM((NZ, 8, 128), F32),
            dma((11,)),
            dma((2,)), dma((2,)), dma((2,)), dma((2,)),
            dma((2,)), dma((2,)), dma((2,)), dma((2,)),
            dma(()), dma((16, 2)), dma(()), dma((16, 2)),
            dma(()), dma((16,)),
            dma((16,)), dma(()),
            dma((4,)), dma((4,)),
        ],
        compiler_params=pltpu.CompilerParams(
            collective_id=0, has_side_effects=True, vmem_limit_bytes=56 * 1024 * 1024
        ),
    )(dwa_coefs, layer_outs, avg_grads, attn_mixed)


def solution(mesh):
    in_specs = (P(None, "dp", "tensor"), P(None, "dp", "tensor"), P("dp", "tensor"), P())
    out_specs = (P(), P("dp", "tensor"))
    return jax.shard_map(local, mesh=mesh, in_specs=in_specs, out_specs=out_specs, check_vma=False)
```

time: 197 us -> 78.5 us (0.40); the launches traced: 194 us -> 78 us
  waiting for transfers between devices: 118 us -> 0 us
  Pallas kernels: 0 us -> 74.5 us
  matrix products: 21.7 us -> 0 us
  starting transfers between devices: 21.7 us -> 0 us
  between operations: 14.1 us -> 0.64 us
  other arithmetic: 7.86 us -> 0 us
  blocking collectives: 7.57 us -> 0 us
    all_to_all x2 -> x0, waiting for transfers between devices: 95.4 us -> none  [the longest x1 95.4 us: sum_at_owner(): parts = lax.all_to_all(split_up(value, dim, length), axis, 0, 0, tiled=True)]
    pallas_call x0 -> x1, Pallas kernels: none -> 74.5 us  [local(): pl.pallas_call(kernel, out_shape=(jax.ShapeDtypeStruct((4, 5), F32), jax....]
    all_gather x1 -> x0, waiting for transfers between devices: 22.5 us -> none  [weight_grad(): lax.all_gather(out_grad, 'tensor', axis=1, tiled=True)]
    all_to_all x2 -> x0, starting transfers between devices: 21.7 us -> none  [the longest x1 11.7 us: copy_for_each(): lax.all_to_all(jnp.broadcast_to(value[None], (length, *value.shape)), axi...]
    dot_general x2 -> x0, matrix products: 21.7 us -> none  [the longest x1 12 us: coef_partial(): lax.dot_general(grads_flat, outs_flat, (((1,), (1,)), ((), ())), preferre...]
    all_to_all x1 -> x0, blocking collectives: 7.57 us -> none  [copy_for_each(): lax.all_to_all(jnp.broadcast_to(value[None], (length, *value.shape)), axi...]
    convert_element_type x1 -> x0, other arithmetic: 4.28 us -> none  [weight_grad(): out_grad = (first + second).astype(jnp.bfloat16)]
    reduce_sum x3 -> x0, other arithmetic: 3.57 us -> none  [the longest x1 3.5 us: sum_at_owner(): return jnp.sum(parts.astype(jnp.float32), axis=0)]
  transfers between devices with their start and end apart: 3 -> 0, of which waited for: 2 -> 0; matrix products, arithmetic and copies ran while one was open for 12% -> 0% of each run, Pallas kernels for 0% -> 0%
where the time goes in v1:
time: 78.5 us; the launch traced here: 78 us
  Pallas kernels  74.5 us (95%)
  local copies, waits for them, and re-layouts  2.92 us (4%)
    pallas_call x1, Pallas kernels, local(): pl.pallas_call(kernel, out_shape=(jax.ShapeDtypeStruct((4, 5), F32), jax....  74.5 us
    unnamed x2, local copies, waits for them, and re-layouts  2.92 us

profile of v1, /device:TPU:4, one launch (start us, length us, event | category | flops | bytes accessed | tf_op | source)
XLA Modules:
  0.0 78.0 jit_solution(11902769066548984415)
XLA Ops:
  0.6 74.5 %shard_map.59 = (f32[4,5]{1,0:T(4,128)}, f32[128,512]{1,0:T(8,128)}) custom-call(f32[4,5]{1,0:T(4,128)} %co.1, bf16[5,1024,512]{2,1,0:T(8,128)(2,1)} %lo_h.1, bf16[4,1024,512]{2,1,0:T(8,128)(2,1)} %ag_h.1, bf16[1024,512]{1,0:T(8,128)(2,1)} %at_h.1), custom_call_target="tpu_custom_call" | custom-call | tf_op jit(solution)/shard_map/pallas_call | solution.py:314
  75.1 1.2 %copy.8 = f32[4,5]{1,0:T(4,128)} copy(f32[4,5]{1,0:T(4,128)} %get-tuple-element.4) | data formatting | bytes 160
  76.3 1.7 %copy.9 = f32[128,512]{1,0:T(8,128)} copy(f32[128,512]{1,0:T(8,128)} %get-tuple-element.5) | data formatting | bytes 524288

commit v2 on v1

v2 whole, which is shorter than its diff:
```python
import jax
import jax.numpy as jnp
from jax import lax
from jax.experimental import pallas as pl
from jax.experimental.pallas import tpu as pltpu
from jax.sharding import PartitionSpec as P

MESH = pl.DeviceIdType.MESH
F32, BF16 = jnp.float32, jnp.bfloat16
NX, NY, NZ = 4, 4, 8
PAIRS_Z = [(1, 1), (0, 2), (0, 3), (1, 3)]
PAIRS_Y = [(0, 0), (0, 1), (1, 0), (1, 2), (2, 0), (2, 1), (2, 2), (2, 3), (3, 0), (3, 1), (3, 2), (3, 3)]
PAIRS = [(i, j) for i in range(4) for j in range(5) if j <= i + 1]


def kernel(
    co, lo_h, ag_h, at_h, coef_out, proj_out,
    lo, ag, ab, gt, outb, cb_c, cb_x, cb_y, cb_z,
    in_sem, gd_s, gd_r, gx_s, gx_r, gf_s, gf_r, ax_s, ax_r, f_r, c_s, c_r,
    *sums,
):
    dp, tk = lax.axis_index("dp"), lax.axis_index("tensor")
    z, y = dp // NY, dp % NY
    x, c = tk // 2, tk % 2
    xg = x + 1 - 2 * (x % 2)
    xa = NX - 1 - x

    def dev(x_, y_, z_, c_):
        return (z_ * NY + y_, x_ * 2 + c_)

    def send(src, dst, send_sem, recv_sem, where):
        copy = pltpu.make_async_remote_copy(
            src_ref=src, dst_ref=dst, send_sem=send_sem, recv_sem=recv_sem,
            device_id=where, device_id_type=MESH,
        )
        copy.start()

    def arrived(ref, sem):
        pltpu.make_async_copy(ref, ref, sem).wait()

    others_x = [(x + k) % NX for k in range(1, NX)]
    others_y = [(y + k) % NY for k in range(1, NY)]
    others_z = [(z + k) % NZ for k in range(1, NZ)]

    loads = {}

    def load(name, src, dst, i):
        loads[name] = pltpu.make_async_copy(src, dst, in_sem.at[i])
        loads[name].start()

    for part in range(2):
        rows = pl.ds(part * 512, 512)
        load(f"ag2{part}", ag_h.at[2, rows], ag.at[2, rows], part)
        load(f"ag3{part}", ag_h.at[3, rows], ag.at[3, rows], 11 + part)
    load("ab0", at_h.at[:, pl.ds(0, 256)], ab.at[0], 2)
    load("ab1", at_h.at[:, pl.ds(256, 256)], ab.at[1], 3)
    load("ag0", ag_h.at[0], ag.at[0], 4)
    load("ag1", ag_h.at[1], ag.at[1], 5)
    for j in range(5):
        load(f"lo{j}", lo_h.at[j], lo.at[j], 6 + j)

    barrier = pltpu.get_barrier_semaphore()
    greeted = [dev(x, y, z, 1 - c)]
    greeted += [dev(x_, y, z, c) for x_ in others_x]
    greeted += [dev(x, y_, z, c) for y_ in others_y]
    greeted += [dev(x, y, z_, c) for z_ in others_z]
    greeted += [dev(xa, y, z_, c) for z_ in others_z]
    for where in greeted:
        pl.semaphore_signal(barrier, inc=1, device_id=where, device_id_type=MESH)

    c2, c3 = co[2, 3], co[3, 3]

    def out_grad(i, _):
        rows = pl.ds(pl.multiple_of(i * 256, 256), 256)
        for yy in range(NY):
            cols = pl.ds(yy * 128, 128)
            first = c2 * ag[2, rows, cols].astype(F32)
            second = c3 * ag[3, rows, cols].astype(F32)
            turned = (first + second).astype(BF16).T
            for hh in range(2):
                gt[hh, yy, c, :, rows] = turned[hh * 64 : hh * 64 + 64]
        return 0

    for part in range(2):
        loads[f"ag2{part}"].wait()
        loads[f"ag3{part}"].wait()
        lax.fori_loop(2 * part, 2 * part + 2, out_grad, 0)
    pl.semaphore_wait(barrier, len(greeted))
    for j in range(2):
        send(gt.at[j, :, c], gt.at[j, :, c], gd_s.at[j], gd_r.at[j], dev(x, y, z, 1 - c))
        send(gt.at[j, :, c], gt.at[2 + j, :, c], gx_s.at[j], gx_r.at[j], dev(xg, y, z, c))
        loads[f"ab{j}"].wait()
        send(ab.at[j], ab.at[2 + j], ax_s.at[j], ax_r.at[j], dev(xa, y, z, c))

    up, down = dev(x, (y + 1) % NY, z, c), dev(x, (y + 3) % NY, z, c)

    class Sums:
        def __init__(self, refs):
            (
                self.pf, self.s1, self.r1, self.s2, self.r2, self.zs, self.za, self.zt, self.zb,
                self.out, self.y1_s, self.y1_r, self.y2_s, self.y2_r, self.z1_s, self.za_r,
                self.z2_s, self.zb_r, self.f_s,
            ) = refs

        def y_first(self, b):
            far = self.pf[b, (y + 2) % NY].astype(BF16)
            for i, where in enumerate((up, down)):
                self.s1[b, i] = far[4 * i : 4 * i + 4]
                send(self.s1.at[b, i], self.r1.at[b, i], self.y1_s, self.y1_r.at[b, i], where)

        def y_second(self, b):
            for i, (where, yc) in enumerate(((up, (y + 1) % NY), (down, (y + 3) % NY))):
                arrived(self.r1.at[b, i], self.y1_r.at[b, i])
                both, alone = pl.ds(4 * i, 4), pl.ds(4 - 4 * i, 4)
                self.s2[b, i, both] = (self.pf[b, yc, both] + self.r1[b, i].astype(F32)).astype(BF16)
                self.s2[b, i, alone] = self.pf[b, yc, alone].astype(BF16)
                send(self.s2.at[b, i], self.r2.at[b, i], self.y2_s, self.y2_r.at[b, i], where)

        def z_first(self, b, base):
            arrived(self.r2.at[b, 0], self.y2_r.at[b, 0])
            arrived(self.r2.at[b, 1], self.y2_r.at[b, 1])
            total = self.pf[b, y] + self.r2[b, 0].astype(F32) + self.r2[b, 1].astype(F32)
            self.pf[b, y] = total
            self.zs[b] = total.astype(BF16)
            far = 2 if b % 2 == 0 else 6
            for k, via, buf, n, sem in (
                (4, far, self.za, 2, self.za_r),
                (3, 1, self.za, 0, self.za_r),
                (5, 7, self.za, 1, self.za_r),
                (1, 1, self.zb, 0, self.zb_r),
                (7, 7, self.zb, 1, self.zb_r),
            ):
                src = self.zs.at[b, slot_of(k, base)]
                send(src, buf.at[b, n], self.z1_s, sem.at[b], dev(x, y, (z + via) % NZ, c))

        def z_second(self, b, base):
            arrived(self.za.at[b], self.za_r.at[b])
            for n, k in enumerate((2, 6)):
                part = self.pf[b, y, slot_of(k, base)] + self.za[b, n].astype(F32)
                if b % 2 == n:
                    part = part + self.za[b, 2].astype(F32)
                self.zt[b, n] = part.astype(BF16)
                there = dev(x, y, (z + k) % NZ, c)
                send(self.zt.at[b, n], self.zb.at[b, 2 + n], self.z2_s, self.zb_r.at[b], there)

        def home(self, b, base, own_plane, place):
            arrived(self.zb.at[b], self.zb_r.at[b])
            slot = slot_of(0, base)
            total = self.pf[b, y, slot]
            for k in range(4):
                total = total + self.zb[b, k].astype(F32)
            deliver(total, slot, self.out.at[b], self.f_s.at[b], base, own_plane, place)

        def ends(self, plan):
            arrived(self.s1, self.y1_s)
            arrived(self.s2, self.y2_s)
            arrived(self.zs.at[:, pl.ds(0, 5)], self.z1_s)
            arrived(self.zt, self.z2_s)
            delivered(self.out, self.f_s, plan)

    class SumsZ:
        def __init__(self, refs):
            (
                self.pf, self.zs, self.za, self.zt, self.zb, self.ys, self.yb, self.out,
                self.z1_s, self.za_r, self.z2_s, self.zb_r, self.y_s, self.yb_r, self.f_s,
            ) = refs

        def z_first(self, b, base):
            self.zs[b] = self.pf[b].astype(BF16)
            far = 2 if b % 2 == 0 else 6
            for k, via, buf, n, sem in (
                (4, far, self.za, 2, self.za_r),
                (3, 1, self.za, 0, self.za_r),
                (5, 7, self.za, 1, self.za_r),
                (1, 1, self.zb, 0, self.zb_r),
                (7, 7, self.zb, 1, self.zb_r),
            ):
                src = self.zs.at[b, slot_of(k, base)]
                send(src, buf.at[b, n], self.z1_s, sem.at[b], dev(x, y, (z + via) % NZ, c))

        def z_second(self, b, base):
            arrived(self.za.at[b], self.za_r.at[b])
            for n, k in enumerate((2, 6)):
                part = self.pf[b, slot_of(k, base)] + self.za[b, n].astype(F32)
                if b % 2 == n:
                    part = part + self.za[b, 2].astype(F32)
                self.zt[b, n] = part.astype(BF16)
                there = dev(x, y, (z + k) % NZ, c)
                send(self.zt.at[b, n], self.zb.at[b, 2 + n], self.z2_s, self.zb_r.at[b], there)

        def y_share(self, b, base):
            arrived(self.zb.at[b], self.zb_r.at[b])
            slot = slot_of(0, base)
            total = self.pf[b, slot]
            for k in range(4):
                total = total + self.zb[b, k].astype(F32)
            self.pf[b, slot] = total
            self.ys[b] = total.astype(BF16)
            for k in range(1, NY):
                yc = (y + k) % NY
                send(self.ys.at[b, yc], self.yb.at[b, k - 1], self.y_s, self.yb_r.at[b], dev(x, yc, z, c))

        def home(self, b, base, own_plane, place):
            arrived(self.yb.at[b], self.yb_r.at[b])
            slot = slot_of(0, base)
            total = self.pf[b, slot, y]
            for k in range(3):
                total = total + self.yb[b, k].astype(F32)
            deliver(total, slot, self.out.at[b], self.f_s.at[b], base, own_plane, place)

        def ends(self, plan):
            arrived(self.zs.at[:, pl.ds(0, 5)], self.z1_s)
            arrived(self.zt, self.z2_s)
            arrived(self.yb, self.y_s)
            delivered(self.out, self.f_s, plan)

    def deliver(total, slot, out, sem, base, own_plane, place):
        zh_ = 2 * base + slot // 4
        dst = outb.at[place(slot % 4)]

        def put(ref):
            for n in range(2):
                ref[n] = total[:, 128 * n : 128 * n + 128]

        if own_plane:

            @pl.when(zh_ == z)
            def _():
                put(dst)

            @pl.when(zh_ != z)
            def _():
                put(out)
                send(out, dst, sem, f_r, dev(x, y, zh_, c))

        else:
            put(out)
            send(out, dst, sem, f_r, dev(xa, y, zh_, c))

    def delivered(out, sems, plan):
        for b, (base, own_plane, _) in enumerate(plan):
            if own_plane:

                @pl.when(2 * base + slot_of(0, base) // 4 != z)
                def _():
                    arrived(out.at[b], sems.at[b])

            else:
                arrived(out.at[b], sems.at[b])

    def slot_of(k, base):
        return (z + k - 2 * base + 3 + NZ) % NZ

    ysum, zsum = Sums(sums[:19]), SumsZ(sums[19:])

    def product(g, a, b):
        term = jnp.dot(gt[g].reshape(512, 1024), ab[a], preferred_element_type=F32)
        ysum.pf[b] = term.reshape(NY, 8, 16, 256)
        ysum.y_first(b)

    def product_z(g, a, b):
        term = jnp.dot(gt[g].reshape(512, 1024), ab[a], preferred_element_type=F32)
        term = term.reshape(NY, 8, 16, 256)
        for yc in range(NY):
            zsum.pf[b, :, yc] = term[yc]
        zsum.z_first(b, plan_z[b][0])

    def loop(count, fn):
        def step(t, _):
            fn(t)
            return 0

        lax.fori_loop(0, count, step, 0)

    def plan_of(pairs):
        def place(g, a):
            return lambda u: (g % 2 * 4 + u, pl.ds(a % 2 * 2, 2))

        return [(x if g < 2 else xg, a < 2, place(g, a)) for g, a in pairs]

    plan_y, plan_z = plan_of(PAIRS_Y), plan_of(PAIRS_Z)

    def zf(*batches):
        for b in batches:
            ysum.z_first(b, plan_y[b][0])

    def zs(*batches):
        for b in batches:
            ysum.z_second(b, plan_y[b][0])

    def zh(*batches):
        for b in batches:
            ysum.home(b, *plan_y[b])

    def y2(*batches):
        for b in batches:
            ysum.y_second(b)

    def zz(b):
        zsum.z_second(b, plan_z[b][0])

    def zy(b):
        zsum.y_share(b, plan_z[b][0])

    def zn(b):
        zsum.home(b, *plan_z[b])

    def pass_on(j):
        src = gt.at[2 + j, :, c]
        arrived(src, gx_r.at[j])
        send(src, src, gf_s.at[j], gf_r.at[j], dev(x, y, z, 1 - c))

    def passed_on(j):
        arrived(gt.at[2 + j, :, 1 - c], gf_r.at[j])

    def coef_step(r, accs):
        rows = pl.ds(pl.multiple_of(r * 16, 16), 16)
        accs = list(accs)
        for q in range(4):
            cols = pl.ds(q * 128, 128)
            outs = [lo[j, rows, cols].astype(F32) for j in range(5)]
            grads = [ag[i, rows, cols].astype(F32) for i in range(4)]
            for n, (i, j) in enumerate(PAIRS):
                p = grads[i] * outs[j]
                accs[n] = accs[n] + (p[:8] + p[8:])
        return tuple(accs)

    def spread(buf, own, k0, targets, stage, size):
        for k, where in enumerate(targets):
            send(buf.at[own], buf.at[own], c_s.at[stage], c_r.at[stage], where)

    def settle(buf, own, stage, size):
        arrived(buf.at[pl.ds(0, size - 1)], c_r.at[stage])
        total = buf[0]
        for k in range(1, size):
            total = total + buf[k]
        return total

    def coef_local():
        for name in ["ag0", "ag1"] + [f"lo{j}" for j in range(5)]:
            loads[name].wait()
        zero = jnp.zeros((8, 128), F32)
        accs = lax.fori_loop(0, 64, coef_step, (zero,) * len(PAIRS))
        row = lax.broadcasted_iota(jnp.int32, (8, 128), 0)
        col = lax.broadcasted_iota(jnp.int32, (8, 128), 1)
        tile = zero
        for n, (i, j) in enumerate(PAIRS):
            total = jnp.sum(jnp.sum(accs[n], axis=0, keepdims=True), axis=1, keepdims=True)
            tile = jnp.where((row == i) & (col == j), jnp.broadcast_to(total, (8, 128)), tile)
        cb_c[c] = tile
        spread(cb_c, c, 0, [dev(x, y, z, 1 - c)], 0, 2)

    def coef_x():
        cb_x[x] = settle(cb_c, c, 0, 2)
        spread(cb_x, x, 0, [dev(x_, y, z, c) for x_ in others_x], 1, NX)

    def coef_y():
        cb_y[y] = settle(cb_x, x, 1, NX)
        spread(cb_y, y, 0, [dev(x, y_, z, c) for y_ in others_y], 2, NY)

    def coef_z():
        cb_z[z] = settle(cb_y, y, 2, NY)
        spread(cb_z, z, 0, [dev(x, y, z_, c) for z_ in others_z], 3, NZ)

    for j in range(2):
        arrived(gt.at[j, :, 1 - c], gd_r.at[j])
    product_z(1, 1, 0)
    loop(3, lambda t: product(t // 2, t % 2, t))
    y2(0, 1, 2)
    coef_local()
    zz(0)
    zf(0)

    arrived(ab.at[2], ax_r.at[0])
    pass_on(0)
    product_z(0, 2, 1)
    product(1, 2, 3)
    passed_on(0)
    loop(3, lambda t: product(2, t, 4 + t))
    zf(1, 2)
    y2(3)
    zs(0)
    y2(4)
    coef_x()
    y2(5, 6)
    zy(0)
    zs(1, 2)
    zz(1)
    zf(3)

    arrived(ab.at[3], ax_r.at[1])
    pass_on(1)
    product(2, 3, 7)
    product_z(0, 3, 2)
    product_z(1, 3, 3)
    passed_on(1)
    loop(4, lambda t: product(3, t, 8 + t))
    coef_y()
    zf(4, 5, 6)
    y2(7, 8, 9, 10, 11)
    zh(0, 1, 2)
    zn(0)
    zs(3, 4, 5, 6)
    zz(2)
    zf(7)
    coef_z()
    zz(3)
    zf(8)
    zh(3, 4)
    zf(9)
    zs(7)
    zh(5, 6)
    zf(10)
    zs(8)
    zy(1)
    zf(11)
    zs(9)
    zy(2)
    zh(7)
    zy(3)
    zs(10)
    zh(8)
    zs(11)
    zh(9)
    zn(1)
    zn(2)
    coef_out[...] = settle(cb_z, z, 3, NZ)
    zh(10)
    zn(3)
    zh(11)

    at_home = z // 4 == x // 2

    @pl.when(at_home)
    def _():
        arrived(outb.at[pl.ds(0, 6)], f_r)

    @pl.when(jnp.logical_not(at_home))
    def _():
        arrived(outb, f_r)

    proj_out[...] = outb[...]

    ysum.ends(plan_y)
    zsum.ends(plan_z)
    arrived(cb_c.at[0], c_s.at[0])
    arrived(cb_x.at[pl.ds(0, NX - 1)], c_s.at[1])
    arrived(cb_y.at[pl.ds(0, NY - 1)], c_s.at[2])
    arrived(cb_z.at[pl.ds(0, NZ - 1)], c_s.at[3])
    for j in range(2):
        arrived(ab.at[j], ax_s.at[j])
        arrived(gt.at[j, :, c], gx_s.at[j])
        arrived(gt.at[j, :, c], gd_s.at[j])
        arrived(gt.at[2 + j, :, c], gf_s.at[j])


OUT_COEF, OUT_PROJ = pltpu.VMEM((8, 128), F32), pltpu.VMEM((8, 4, 16, 128), F32)


def sums_scratch(count, width):
    dma = pltpu.SemaphoreType.DMA
    return [
        pltpu.VMEM((count, NY, 8, 16, width), F32),
        pltpu.VMEM((count, 2, 4, 16, width), BF16),
        pltpu.VMEM((count, 2, 4, 16, width), BF16),
        pltpu.VMEM((count, 2, 8, 16, width), BF16),
        pltpu.VMEM((count, 2, 8, 16, width), BF16),
        pltpu.VMEM((count, 8, 16, width), BF16),
        pltpu.VMEM((count, 3, 16, width), BF16),
        pltpu.VMEM((count, 2, 16, width), BF16),
        pltpu.VMEM((count, 4, 16, width), BF16),
        pltpu.VMEM((count, width // 128, 16, 128), F32),
        dma(()), dma((count, 2)), dma(()), dma((count, 2)),
        dma(()), dma((count,)), dma(()), dma((count,)),
        dma((count,)),
    ]


def sums_z_scratch(count):
    dma = pltpu.SemaphoreType.DMA
    return [
        pltpu.VMEM((count, 8, NY, 16, 256), F32),
        pltpu.VMEM((count, 8, NY, 16, 256), BF16),
        pltpu.VMEM((count, 3, NY, 16, 256), BF16),
        pltpu.VMEM((count, 2, NY, 16, 256), BF16),
        pltpu.VMEM((count, 4, NY, 16, 256), BF16),
        pltpu.VMEM((count, NY, 16, 256), BF16),
        pltpu.VMEM((count, 3, 16, 256), BF16),
        pltpu.VMEM((count, 2, 16, 128), F32),
        dma(()), dma((count,)), dma(()), dma((count,)),
        dma(()), dma((count,)), dma((count,)),
    ]


def local(layer_outs, avg_grads, attn_mixed, dwa_coefs):
    dma = pltpu.SemaphoreType.DMA
    anywhere = pl.BlockSpec(memory_space=pl.ANY)
    vmem = pl.BlockSpec(memory_space=pltpu.VMEM)
    coef, proj = pl.pallas_call(
        kernel,
        out_shape=(OUT_COEF, OUT_PROJ),
        in_specs=[pl.BlockSpec(memory_space=pltpu.SMEM), anywhere, anywhere, anywhere],
        out_specs=(vmem, vmem),
        scratch_shapes=[
            pltpu.VMEM((5, 1024, 512), BF16),
            pltpu.VMEM((4, 1024, 512), BF16),
            pltpu.VMEM((4, 1024, 256), BF16),
            pltpu.VMEM((4, NY, 2, 64, 1024), BF16),
            pltpu.VMEM((8, 4, 16, 128), F32),
            pltpu.VMEM((2, 8, 128), F32),
            pltpu.VMEM((NX, 8, 128), F32),
            pltpu.VMEM((NY, 8, 128), F32),
            pltpu.VMEM((NZ, 8, 128), F32),
            dma((13,)),
            dma((2,)), dma((2,)), dma((2,)), dma((2,)),
            dma((2,)), dma((2,)), dma((2,)), dma((2,)),
            dma(()), dma((4,)), dma((4,)),
            *sums_scratch(len(PAIRS_Y), 256),
            *sums_z_scratch(len(PAIRS_Z)),
        ],
        compiler_params=pltpu.CompilerParams(
            collective_id=0, has_side_effects=True, vmem_limit_bytes=56 * 1024 * 1024
        ),
    )(dwa_coefs, layer_outs, avg_grads, attn_mixed)
    coef = pltpu.with_memory_space_constraint(coef, pltpu.VMEM)
    proj = pltpu.with_memory_space_constraint(proj, pltpu.VMEM)
    return pl.pallas_call(
        lay_out,
        out_shape=(jax.ShapeDtypeStruct((4, 5), F32), jax.ShapeDtypeStruct((128, 512), F32)),
        in_specs=[vmem, vmem],
        out_specs=(vmem, vmem),
    )(coef, proj)


def lay_out(coef, proj, coef_out, proj_out):
    coef_out[...] = coef[:4, :5]
    for block in range(8):
        for j in range(4):
            proj_out[pl.ds(block * 16, 16), pl.ds(j * 128, 128)] = proj[block, j]


def solution(mesh):
    in_specs = (P(None, "dp", "tensor"), P(None, "dp", "tensor"), P("dp", "tensor"), P())
    out_specs = (P(), P("dp", "tensor"))
    return jax.shard_map(local, mesh=mesh, in_specs=in_specs, out_specs=out_specs, check_vma=False)
```

time: 78.5 us -> 70.7 us (0.901)
  Pallas kernels: 74.5 us -> 70 us
  local copies, waits for them, and re-layouts: 2.92 us -> 0 us
    pallas_call x1 -> x2, Pallas kernels: 74.5 us -> 70 us  [the longest x1 69.3 us: local(): pl.pallas_call(kernel, out_shape=(OUT_COEF, OUT_PROJ), in_specs=[pl.Block...]
    unnamed x2 -> x0, local copies, waits for them, and re-layouts: 2.92 us -> none
where the time goes in v2:
time: 70.7 us; the launch traced here: 70.6 us
  Pallas kernels  70 us (99%)
    pallas_call x1, Pallas kernels, local(): pl.pallas_call(kernel, out_shape=(OUT_COEF, OUT_PROJ), in_specs=[pl.Block...  69.3 us

profile of v2, /device:TPU:4, one launch (start us, length us, event | category | flops | bytes accessed | tf_op | source)
XLA Modules:
  0.0 70.6 jit_solution(10146750657829891139)
XLA Ops:
  0.6 69.3 %shard_map.59 = (f32[8,128]{1,0:T(8,128)S(1)}, f32[8,4,16,128]{3,2,1,0:T(8,128)S(1)}) custom-call(f32[4,5]{1,0:T(4,128)} %co.1, bf16[5,1024,512]{2,1,0:T(8,128)(2,1)} %lo_h.1, bf16[4,1024,512]{2,1,0:T(8,128)(2,1)} %ag_h.1, bf16[1024,512]{1,0:T(8,128)(2,1)} %at_h.1), custom_call_target="tpu_custom_call" | custom-call | tf_op jit(solution)/shard_map/pallas_call | solution.py:499
  69.9 0.7 %shard_map.60 = (f32[4,5]{1,0:T(4,128)}, f32[128,512]{1,0:T(8,128)}) custom-call(f32[8,128]{1,0:T(8,128)S(1)} %get-tuple-element.4.coef, f32[8,4,16,128]{3,2,1,0:T(8,128)S(1)} %get-tuple-element.5.proj), custom_call_target="tpu_custom_call" | custom-call | tf_op jit(solution)/shard_map/pallas_call | solution.py:527

commit v3 on v2

--- a/solution.py
+++ b/solution.py
@@ -8,8 +8,9 @@
 MESH = pl.DeviceIdType.MESH
 F32, BF16 = jnp.float32, jnp.bfloat16
 NX, NY, NZ = 4, 4, 8
-PAIRS_Z = [(1, 1), (0, 2), (0, 3), (1, 3)]
-PAIRS_Y = [(0, 0), (0, 1), (1, 0), (1, 2), (2, 0), (2, 1), (2, 2), (2, 3), (3, 0), (3, 1), (3, 2), (3, 3)]
+PAIRS_Z = [(1, 1), (0, 2), (1, 2), (3, 3)]
+PAIRS_Y = [(0, 0), (0, 1), (1, 0), (2, 0), (2, 1), (2, 2), (3, 2), (3, 1), (3, 0)]
+HALVES = [(g, t) for t in range(2) for g in range(3)]
 PAIRS = [(i, j) for i in range(4) for j in range(5) if j <= i + 1]
 
 
@@ -68,6 +69,9 @@
     for where in greeted:
         pl.semaphore_signal(barrier, inc=1, device_id=where, device_id_type=MESH)
 
+    def ab_piece(n, j):
+        return ab.at[n] if j == 0 else ab.at[n + 1, :, pl.ds(128 * (j - 1), 128)]
+
     c2, c3 = co[2, 3], co[3, 3]
 
     def out_grad(i, _):
@@ -90,7 +94,8 @@
         send(gt.at[j, :, c], gt.at[j, :, c], gd_s.at[j], gd_r.at[j], dev(x, y, z, 1 - c))
         send(gt.at[j, :, c], gt.at[2 + j, :, c], gx_s.at[j], gx_r.at[j], dev(xg, y, z, c))
         loads[f"ab{j}"].wait()
-        send(ab.at[j], ab.at[2 + j], ax_s.at[j], ax_r.at[j], dev(xa, y, z, c))
+        for n in ((0,), (1, 2))[j]:
+            send(ab_piece(0, n), ab_piece(2, n), ax_s.at[n], ax_r.at[n], dev(xa, y, z, c))
 
     up, down = dev(x, (y + 1) % NY, z, c), dev(x, (y + 3) % NY, z, c)
 
@@ -219,8 +224,8 @@
         dst = outb.at[place(slot % 4)]
 
         def put(ref):
-            for n in range(2):
-                ref[n] = total[:, 128 * n : 128 * n + 128]
+            for n in range(total.shape[1] // 128):
+                ref[n] = total[:, 128 * n : 128 * n + 128].astype(BF16)
 
         if own_plane:
 
@@ -251,12 +256,18 @@
     def slot_of(k, base):
         return (z + k - 2 * base + 3 + NZ) % NZ
 
-    ysum, zsum = Sums(sums[:19]), SumsZ(sums[19:])
+    ysum, half, zsum = Sums(sums[:19]), Sums(sums[19:38]), SumsZ(sums[38:])
 
     def product(g, a, b):
         term = jnp.dot(gt[g].reshape(512, 1024), ab[a], preferred_element_type=F32)
         ysum.pf[b] = term.reshape(NY, 8, 16, 256)
         ysum.y_first(b)
+
+    def product_half(g, t, b):
+        right = ab[3, :, t * 128 : t * 128 + 128]
+        term = jnp.dot(gt[g].reshape(512, 1024), right, preferred_element_type=F32)
+        half.pf[b] = term.reshape(NY, 8, 16, 128)
+        half.y_first(b)
 
     def product_z(g, a, b):
         term = jnp.dot(gt[g].reshape(512, 1024), ab[a], preferred_element_type=F32)
@@ -278,7 +289,11 @@
 
         return [(x if g < 2 else xg, a < 2, place(g, a)) for g, a in pairs]
 
+    def half_place(g, t):
+        return lambda u: (g % 2 * 4 + u, pl.ds(2 + t, 1))
+
     plan_y, plan_z = plan_of(PAIRS_Y), plan_of(PAIRS_Z)
+    plan_half = [(x if g < 2 else xg, False, half_place(g, t)) for g, t in HALVES]
 
     def zf(*batches):
         for b in batches:
@@ -295,6 +310,22 @@
     def y2(*batches):
         for b in batches:
             ysum.y_second(b)
+
+    def hf(*batches):
+        for b in batches:
+            half.z_first(b, plan_half[b][0])
+
+    def hs(*batches):
+        for b in batches:
+            half.z_second(b, plan_half[b][0])
+
+    def hh(*batches):
+        for b in batches:
+            half.home(b, *plan_half[b])
+
+    def h2(*batches):
+        for b in batches:
+            half.y_second(b)
 
     def zz(b):
         zsum.z_second(b, plan_z[b][0])
@@ -371,63 +402,68 @@
     zz(0)
     zf(0)
 
-    arrived(ab.at[2], ax_r.at[0])
+    arrived(ab_piece(2, 0), ax_r.at[0])
     pass_on(0)
     product_z(0, 2, 1)
-    product(1, 2, 3)
+    product_z(1, 2, 2)
     passed_on(0)
-    loop(3, lambda t: product(2, t, 4 + t))
+    loop(3, lambda t: product(2, t, 3 + t))
     zf(1, 2)
-    y2(3)
     zs(0)
-    y2(4)
+
+    arrived(ab_piece(2, 1), ax_r.at[1])
+    loop(3, lambda t: product_half(t, 0, t))
     coef_x()
-    y2(5, 6)
+    y2(3, 4, 5)
     zy(0)
     zs(1, 2)
     zz(1)
-    zf(3)
-
-    arrived(ab.at[3], ax_r.at[1])
+    h2(0, 1, 2)
+    zz(2)
+
+    arrived(ab_piece(2, 2), ax_r.at[2])
     pass_on(1)
-    product(2, 3, 7)
-    product_z(0, 3, 2)
-    product_z(1, 3, 3)
+    loop(3, lambda t: product_half(t, 1, 3 + t))
+    zf(3, 4)
     passed_on(1)
-    loop(4, lambda t: product(3, t, 8 + t))
+    product_z(3, 3, 3)
+    loop(3, lambda t: product(3, 2 - t, 6 + t))
     coef_y()
-    zf(4, 5, 6)
-    y2(7, 8, 9, 10, 11)
+    zf(5)
+    h2(3, 4, 5)
+    hf(0, 1)
+    y2(6)
+    hf(2)
+    y2(7, 8)
+    zs(3, 4, 5)
     zh(0, 1, 2)
     zn(0)
-    zs(3, 4, 5, 6)
-    zz(2)
+    zy(1)
+    zy(2)
+    hs(0, 1)
+    hf(3)
+    zz(3)
+    hf(4, 5)
+    hs(2)
+    coef_z()
+    zf(6)
+    zh(3, 4, 5)
     zf(7)
-    coef_z()
-    zz(3)
+    hs(3, 4)
     zf(8)
-    zh(3, 4)
-    zf(9)
+    hh(0, 1, 2)
+    hs(5)
+    zs(6)
+    zy(3)
     zs(7)
-    zh(5, 6)
-    zf(10)
+    hh(3, 4, 5)
     zs(8)
-    zy(1)
-    zf(11)
-    zs(9)
-    zy(2)
-    zh(7)
-    zy(3)
-    zs(10)
-    zh(8)
-    zs(11)
-    zh(9)
     zn(1)
     zn(2)
     coef_out[...] = settle(cb_z, z, 3, NZ)
-    zh(10)
+    zh(6, 7)
     zn(3)
-    zh(11)
+    zh(8)
 
     at_home = z // 4 == x // 2
 
@@ -442,19 +478,21 @@
     proj_out[...] = outb[...]
 
     ysum.ends(plan_y)
+    half.ends(plan_half)
     zsum.ends(plan_z)
     arrived(cb_c.at[0], c_s.at[0])
     arrived(cb_x.at[pl.ds(0, NX - 1)], c_s.at[1])
     arrived(cb_y.at[pl.ds(0, NY - 1)], c_s.at[2])
     arrived(cb_z.at[pl.ds(0, NZ - 1)], c_s.at[3])
     for j in range(2):
-        arrived(ab.at[j], ax_s.at[j])
         arrived(gt.at[j, :, c], gx_s.at[j])
         arrived(gt.at[j, :, c], gd_s.at[j])
         arrived(gt.at[2 + j, :, c], gf_s.at[j])
-
-
-OUT_COEF, OUT_PROJ = pltpu.VMEM((8, 128), F32), pltpu.VMEM((8, 4, 16, 128), F32)
+    for j in range(3):
+        arrived(ab_piece(0, j), ax_s.at[j])
+
+
+OUT_COEF, OUT_PROJ = pltpu.VMEM((8, 128), F32), pltpu.VMEM((8, 4, 16, 128), BF16)
 
 
 def sums_scratch(count, width):
@@ -469,7 +507,7 @@
         pltpu.VMEM((count, 3, 16, width), BF16),
         pltpu.VMEM((count, 2, 16, width), BF16),
         pltpu.VMEM((count, 4, 16, width), BF16),
-        pltpu.VMEM((count, width // 128, 16, 128), F32),
+        pltpu.VMEM((count, width // 128, 16, 128), BF16),
         dma(()), dma((count, 2)), dma(()), dma((count, 2)),
         dma(()), dma((count,)), dma(()), dma((count,)),
         dma((count,)),
@@ -486,7 +524,7 @@
         pltpu.VMEM((count, 4, NY, 16, 256), BF16),
         pltpu.VMEM((count, NY, 16, 256), BF16),
         pltpu.VMEM((count, 3, 16, 256), BF16),
-        pltpu.VMEM((count, 2, 16, 128), F32),
+        pltpu.VMEM((count, 2, 16, 128), BF16),
         dma(()), dma((count,)), dma(()), dma((count,)),
         dma(()), dma((count,)), dma((count,)),
     ]
@@ -506,16 +544,17 @@
             pltpu.VMEM((4, 1024, 512), BF16),
             pltpu.VMEM((4, 1024, 256), BF16),
             pltpu.VMEM((4, NY, 2, 64, 1024), BF16),
-            pltpu.VMEM((8, 4, 16, 128), F32),
+            pltpu.VMEM((8, 4, 16, 128), BF16),
             pltpu.VMEM((2, 8, 128), F32),
             pltpu.VMEM((NX, 8, 128), F32),
             pltpu.VMEM((NY, 8, 128), F32),
             pltpu.VMEM((NZ, 8, 128), F32),
             dma((13,)),
             dma((2,)), dma((2,)), dma((2,)), dma((2,)),
-            dma((2,)), dma((2,)), dma((2,)), dma((2,)),
+            dma((2,)), dma((2,)), dma((3,)), dma((3,)),
             dma(()), dma((4,)), dma((4,)),
             *sums_scratch(len(PAIRS_Y), 256),
+            *sums_scratch(len(HALVES), 128),
             *sums_z_scratch(len(PAIRS_Z)),
         ],
         compiler_params=pltpu.CompilerParams(
@@ -536,7 +575,7 @@
     coef_out[...] = coef[:4, :5]
     for block in range(8):
         for j in range(4):
-            proj_out[pl.ds(block * 16, 16), pl.ds(j * 128, 128)] = proj[block, j]
+            proj_out[pl.ds(block * 16, 16), pl.ds(j * 128, 128)] = proj[block, j].astype(F32)
 
 
 def solution(mesh):

time: 70.7 us -> 66.2 us (0.936)
  the two profiles are of different devices: /device:TPU:4 before, /device:TPU:64 now
where the time goes in v3:
time: 66.2 us; the launch traced here: 66.1 us
  Pallas kernels  65.4 us (99%)
    pallas_call x1, Pallas kernels, local(): pl.pallas_call(kernel, out_shape=(OUT_COEF, OUT_PROJ), in_specs=[pl.Block...  64.7 us

profile of v3, /device:TPU:64, one launch (start us, length us, event | category | flops | bytes accessed | tf_op | source)
XLA Modules:
  0.0 66.1 jit_solution(2075418593384739443)
XLA Ops:
  0.6 64.7 %shard_map.59 = (f32[8,128]{1,0:T(8,128)S(1)}, bf16[8,4,16,128]{3,2,1,0:T(8,128)(2,1)S(1)}) custom-call(f32[4,5]{1,0:T(4,128)} %co.1, bf16[5,1024,512]{2,1,0:T(8,128)(2,1)} %lo_h.1, bf16[4,1024,512]{2,1,0:T(8,128)(2,1)} %ag_h.1, bf16[1024,512]{1,0:T(8,128)(2,1)} %at_h.1), custom_call_target="tpu_custom_call" | custom-call | tf_op jit(solution)/shard_map/pallas_call | solution.py:537
  65.3 0.7 %shard_map.60 = (f32[4,5]{1,0:T(4,128)}, f32[128,512]{1,0:T(8,128)}) custom-call(f32[8,128]{1,0:T(8,128)S(1)} %get-tuple-element.4.coef, bf16[8,4,16,128]{3,2,1,0:T(8,128)(2,1)S(1)} %get-tuple-element.5.proj), custom_call_target="tpu_custom_call" | custom-call | tf_op jit(solution)/shard_map/pallas_call | solution.py:566

commit v4 on v3

--- a/solution.py
+++ b/solution.py
@@ -8,8 +8,8 @@
 MESH = pl.DeviceIdType.MESH
 F32, BF16 = jnp.float32, jnp.bfloat16
 NX, NY, NZ = 4, 4, 8
-PAIRS_Z = [(1, 1), (0, 2), (1, 2), (3, 3)]
-PAIRS_Y = [(0, 0), (0, 1), (1, 0), (2, 0), (2, 1), (2, 2), (3, 2), (3, 1), (3, 0)]
+PAIRS_Z = [(1, 1), (0, 2), (1, 2), (2, 2), (3, 3)]
+PAIRS_Y = [(0, 0), (0, 1), (1, 0), (2, 0), (2, 1), (3, 2), (3, 1), (3, 0)]
 HALVES = [(g, t) for t in range(2) for g in range(3)]
 PAIRS = [(i, j) for i in range(4) for j in range(5) if j <= i + 1]
 
@@ -407,18 +407,19 @@
     product_z(0, 2, 1)
     product_z(1, 2, 2)
     passed_on(0)
-    loop(3, lambda t: product(2, t, 3 + t))
+    product_z(2, 2, 3)
+    loop(2, lambda t: product(2, t, 3 + t))
     zf(1, 2)
     zs(0)
 
     arrived(ab_piece(2, 1), ax_r.at[1])
     loop(3, lambda t: product_half(t, 0, t))
     coef_x()
-    y2(3, 4, 5)
+    y2(3, 4)
     zy(0)
-    zs(1, 2)
     zz(1)
     h2(0, 1, 2)
+    zs(1, 2)
     zz(2)
 
     arrived(ab_piece(2, 2), ax_r.at[2])
@@ -426,44 +427,40 @@
     loop(3, lambda t: product_half(t, 1, 3 + t))
     zf(3, 4)
     passed_on(1)
-    product_z(3, 3, 3)
-    loop(3, lambda t: product(3, 2 - t, 6 + t))
+    product_z(3, 3, 4)
+    loop(3, lambda t: product(3, 2 - t, 5 + t))
     coef_y()
-    zf(5)
     h2(3, 4, 5)
+    zz(3)
     hf(0, 1)
-    y2(6)
+    y2(5)
     hf(2)
-    y2(7, 8)
-    zs(3, 4, 5)
+    y2(6, 7)
+    zs(3, 4)
     zh(0, 1, 2)
     zn(0)
     zy(1)
     zy(2)
-    hs(0, 1)
     hf(3)
-    zz(3)
+    zz(4)
     hf(4, 5)
-    hs(2)
+    hs(0, 1, 2)
     coef_z()
-    zf(6)
-    zh(3, 4, 5)
-    zf(7)
-    hs(3, 4)
-    zf(8)
-    hh(0, 1, 2)
-    hs(5)
-    zs(6)
+    zf(5, 6, 7)
+    hs(3, 4, 5)
+    zh(3, 4)
+    zs(5, 6)
     zy(3)
+    zy(4)
     zs(7)
-    hh(3, 4, 5)
-    zs(8)
+    hh(0, 1, 2, 3, 4, 5)
     zn(1)
     zn(2)
     coef_out[...] = settle(cb_z, z, 3, NZ)
-    zh(6, 7)
+    zh(5, 6)
     zn(3)
-    zh(8)
+    zn(4)
+    zh(7)
 
     at_home = z // 4 == x // 2
 

time: 66.2 us -> 63.5 us (0.959)
  the two profiles are of different devices: /device:TPU:64 before, /device:TPU:4 now
where the time goes in v4:
time: 63.5 us; the launch traced here: 63.1 us
  Pallas kernels  62.5 us (98%)
  between operations  0.64 us (1%)
    pallas_call x1, Pallas kernels, local(): pl.pallas_call(kernel, out_shape=(OUT_COEF, OUT_PROJ), in_specs=[pl.Block...  61.8 us

profile of v4, /device:TPU:4, one launch (start us, length us, event | category | flops | bytes accessed | tf_op | source)
XLA Modules:
  0.0 63.1 jit_solution(6216723556498628962)
XLA Ops:
  0.6 61.8 %shard_map.59 = (f32[8,128]{1,0:T(8,128)S(1)}, bf16[8,4,16,128]{3,2,1,0:T(8,128)(2,1)S(1)}) custom-call(f32[4,5]{1,0:T(4,128)} %co.1, bf16[5,1024,512]{2,1,0:T(8,128)(2,1)} %lo_h.1, bf16[4,1024,512]{2,1,0:T(8,128)(2,1)} %ag_h.1, bf16[1024,512]{1,0:T(8,128)(2,1)} %at_h.1), custom_call_target="tpu_custom_call" | custom-call | tf_op jit(solution)/shard_map/pallas_call | solution.py:534
  62.4 0.7 %shard_map.60 = (f32[4,5]{1,0:T(4,128)}, f32[128,512]{1,0:T(8,128)}) custom-call(f32[8,128]{1,0:T(8,128)S(1)} %get-tuple-element.4.coef, bf16[8,4,16,128]{3,2,1,0:T(8,128)(2,1)S(1)} %get-tuple-element.5.proj), custom_call_target="tpu_custom_call" | custom-call | tf_op jit(solution)/shard_map/pallas_call | solution.py:563

commit v5 on v4

--- a/solution.py
+++ b/solution.py
@@ -100,7 +100,8 @@
     up, down = dev(x, (y + 1) % NY, z, c), dev(x, (y + 3) % NY, z, c)
 
     class Sums:
-        def __init__(self, refs):
+        def __init__(self, refs, direct=()):
+            self.direct = direct
             (
                 self.pf, self.s1, self.r1, self.s2, self.r2, self.zs, self.za, self.zt, self.zb,
                 self.out, self.y1_s, self.y1_r, self.y2_s, self.y2_r, self.z1_s, self.za_r,
@@ -128,17 +129,24 @@
             self.pf[b, y] = total
             self.zs[b] = total.astype(BF16)
             far = 2 if b % 2 == 0 else 6
-            for k, via, buf, n, sem in (
+            steps = [
                 (4, far, self.za, 2, self.za_r),
                 (3, 1, self.za, 0, self.za_r),
                 (5, 7, self.za, 1, self.za_r),
                 (1, 1, self.zb, 0, self.zb_r),
                 (7, 7, self.zb, 1, self.zb_r),
-            ):
+            ]
+            if b in self.direct:
+                steps = [(k, k, buf, n, sem) for k, _, buf, n, sem in steps]
+                steps += [(2, 2, self.zb, 2, self.zb_r), (6, 6, self.zb, 3, self.zb_r)]
+            for i, (k, via, buf, n, sem) in enumerate(steps):
                 src = self.zs.at[b, slot_of(k, base)]
-                send(src, buf.at[b, n], self.z1_s, sem.at[b], dev(x, y, (z + via) % NZ, c))
+                gone = self.z1_s if i < 5 else self.z2_s
+                send(src, buf.at[b, n], gone, sem.at[b], dev(x, y, (z + via) % NZ, c))
 
         def z_second(self, b, base):
+            if b in self.direct:
+                return
             arrived(self.za.at[b], self.za_r.at[b])
             for n, k in enumerate((2, 6)):
                 part = self.pf[b, y, slot_of(k, base)] + self.za[b, n].astype(F32)
@@ -154,6 +162,10 @@
             total = self.pf[b, y, slot]
             for k in range(4):
                 total = total + self.zb[b, k].astype(F32)
+            if b in self.direct:
+                arrived(self.za.at[b], self.za_r.at[b])
+                for k in range(3):
+                    total = total + self.za[b, k].astype(F32)
             deliver(total, slot, self.out.at[b], self.f_s.at[b], base, own_plane, place)
 
         def ends(self, plan):
@@ -256,7 +268,7 @@
     def slot_of(k, base):
         return (z + k - 2 * base + 3 + NZ) % NZ
 
-    ysum, half, zsum = Sums(sums[:19]), Sums(sums[19:38]), SumsZ(sums[38:])
+    ysum, half, zsum = Sums(sums[:19], (5, 6, 7)), Sums(sums[19:38]), SumsZ(sums[38:])
 
     def product(g, a, b):
         term = jnp.dot(gt[g].reshape(512, 1024), ab[a], preferred_element_type=F32)

time: 63.5 us -> 62.7 us (0.987)
  no operation moved by 1% of the time
where the time goes in v5:
time: 62.7 us; the launch traced here: 62.5 us
  Pallas kernels  61.9 us (99%)
  between operations  0.64 us (1%)
    pallas_call x1, Pallas kernels, local(): pl.pallas_call(kernel, out_shape=(OUT_COEF, OUT_PROJ), in_specs=[pl.Block...  61.2 us

profile of v5, /device:TPU:4, one launch (start us, length us, event | category | flops | bytes accessed | tf_op | source)
XLA Modules:
  0.0 62.5 jit_solution(3890486104551465616)
XLA Ops:
  0.6 61.2 %shard_map.59 = (f32[8,128]{1,0:T(8,128)S(1)}, bf16[8,4,16,128]{3,2,1,0:T(8,128)(2,1)S(1)}) custom-call(f32[4,5]{1,0:T(4,128)} %co.1, bf16[5,1024,512]{2,1,0:T(8,128)(2,1)} %lo_h.1, bf16[4,1024,512]{2,1,0:T(8,128)(2,1)} %ag_h.1, bf16[1024,512]{1,0:T(8,128)(2,1)} %at_h.1), custom_call_target="tpu_custom_call" | custom-call | tf_op jit(solution)/shard_map/pallas_call | solution.py:546
  61.8 0.7 %shard_map.60 = (f32[4,5]{1,0:T(4,128)}, f32[128,512]{1,0:T(8,128)}) custom-call(f32[8,128]{1,0:T(8,128)S(1)} %get-tuple-element.4.coef, bf16[8,4,16,128]{3,2,1,0:T(8,128)(2,1)S(1)} %get-tuple-element.5.proj), custom_call_target="tpu_custom_call" | custom-call | tf_op jit(solution)/shard_map/pallas_call | solution.py:575
